TPU v7x, 32 devices: a whole 2x2x4 slice. The times are simulated.
32 devices in a mesh: batch: 4 (over y, x), ctx: 8 (over z, core).
Axes of the slice: x: 2, y: 2, z: 4, core: 2. Of those that a mesh axis runs over, the one named last changes fastest.
Arguments:
- asked_for: bfloat16 [4, 1024, 64, 64], P('batch', 'ctx'), may hold values from -6 to 6
- offered: bfloat16 [4, 1024, 64, 64], P('batch', 'ctx'), may hold values from -6 to 6
- contents: bfloat16 [4, 1024, 64, 64], P('batch', 'ctx'), may hold values from -6 to 6
- out_weight: bfloat16 [4096, 4096], P('batch'), may hold values from -0.09375 to 0.09375
Outputs:
- layer_out: bfloat16 [4, 1024, 4096], P('batch', 'ctx')
All inputs are finite; a program needn't handle non-finite values.
Results may differ from a plain program's by a relative error of at most 0.006.
Values may be sent and summed in bfloat16 or wider, within the bound.
A program may use at most 128 MiB of HBM per device.

v0:
```python
import jax
import jax.numpy as jnp
from jax import lax
from jax.sharding import PartitionSpec as P


def to_features(values):
    wide = values.astype(jnp.float32)
    return jax.nn.softplus(wide).astype(jnp.bfloat16)


def after_reading(read, count):
    result = read * count**0.5
    return result.astype(jnp.bfloat16)


def look_up(features, state, mass):
    top = jnp.einsum(
        "bthd,bhde->bthe", features, state.astype(jnp.bfloat16), preferred_element_type=jnp.float32
    )
    bottom = jnp.einsum(
        "bthd,bhd->bth", features.astype(jnp.float32), mass, precision=lax.Precision.HIGHEST
    )
    return top / (bottom + 0.001)[..., None]


def shards(asked_for, offered, contents, out_weight):
    query_feature, key_feature = (to_features(asked_for), to_features(offered))
    count = asked_for.shape[1] * lax.axis_size("ctx")
    head_query, head_key, head_value = (
        lax.all_to_all(query_feature, "ctx", split_axis=2, concat_axis=1, tiled=True),
        lax.all_to_all(key_feature, "ctx", split_axis=2, concat_axis=1, tiled=True),
        lax.all_to_all(contents, "ctx", split_axis=2, concat_axis=1, tiled=True),
    )
    state = (
        jnp.einsum("bthd,bthe->bhde", head_key, head_value, preferred_element_type=jnp.float32)
        / count
    )
    mass = jnp.sum(head_key.astype(jnp.float32), axis=1) / count
    head_read = look_up(head_query, state, mass)
    read = lax.all_to_all(head_read, "ctx", split_axis=1, concat_axis=2, tiled=True)
    mixed = after_reading(read, count)
    mixed = mixed.reshape(mixed.shape[0], mixed.shape[1], -1)
    return jnp.einsum(
        "btw,wv->btv",
        mixed,
        lax.all_gather(out_weight, "batch", axis=0, tiled=True),
        preferred_element_type=jnp.float32,
    ).astype(jnp.bfloat16)


def solution(mesh):
    in_specs = (
        P("batch", "ctx", None, None),
        P("batch", "ctx", None, None),
        P("batch", "ctx", None, None),
        P("batch", None),
    )
    out_specs = P("batch", "ctx", None)
    return jax.shard_map(shards, mesh=mesh, in_specs=in_specs, out_specs=out_specs, check_vma=False)
```

profile of v0, /device:TPU:0, one launch (start us, length us, event | category | flops | bytes accessed | tf_op | source)
XLA Modules:
  0.0 329.9 jit_solution(17906474795930241207)
XLA Ops:
  6.5 0.7 all-gather.2.cloned.1.call-update
  7.8 2.2 fusion.10
  10.0 6.5 %all-to-all-start.2 = ((bf16[1,128,64,64]{1,3,0,2:T(8,128)(2,1)}), bf16[1,128,64,64]{1,3,0,2:T(8,128)(2,1)S(1)}, u32[]{:S(2)}, u32[]{:S(2)}) async-start(bf16[1,128,64,64]{1,3,0,2:T(8,128)(2,1)} %fusion.10), calls=%async_computation.2 | async-start | bytes 2097152 | tf_op jit(solution)/shard_map/all_to_all | solution.py:31
  16.4 1.2 fusion.9
  17.7 25.3 %all-to-all-done.2 = bf16[1,128,64,64]{1,3,0,2:T(8,128)(2,1)S(1)} async-done(((bf16[1,128,64,64]{1,3,0,2:T(8,128)(2,1)}), bf16[1,128,64,64]{1,3,0,2:T(8,128)(2,1)S(1)}, u32[]{:S(2)}, u32[]{:S(2)}) %all-to-all-start.2) | async-done | bytes 1048608 | tf_op jit(solution)/shard_map/all_to_all | solution.py:31
  43.0 29.0 %all_to_all.54 = bf16[1,128,64,64]{1,3,0,2:T(8,128)(2,1)S(1)} all-to-all(bf16[1,128,64,64]{1,3,0,2:T(8,128)(2,1)S(1)} %fusion.9), channel_id=1, replica_groups=mesh['batch'=4,'ctx'=8] {'ctx'}, dimensions={2} | all-to-all | bytes 2097152 | tf_op jit(solution)/shard_map/all_to_all | solution.py:32
  72.0 3.6 %all-to-all-start.1 = ((bf16[1,128,64,64]{1,3,0,2:T(8,128)(2,1)}), bf16[1,128,64,64]{1,3,0,2:T(8,128)(2,1)S(1)}, u32[]{:S(2)}, u32[]{:S(2)}) async-start(bf16[1,128,64,64]{1,3,0,2:T(8,128)(2,1)} %bitcast.81), calls=%async_computation.1 | async-start | bytes 2097152 | tf_op jit(solution)/shard_map/all_to_all | solution.py:33
  75.5 1.7 copy.48
  77.2 1.5 reshape.53
  78.8 1.7 copy.50
  80.5 2.3 reshape.51
  82.8 19.3 %all-to-all-done.1 = bf16[1,128,64,64]{1,3,0,2:T(8,128)(2,1)S(1)} async-done(((bf16[1,128,64,64]{1,3,0,2:T(8,128)(2,1)}), bf16[1,128,64,64]{1,3,0,2:T(8,128)(2,1)S(1)}, u32[]{:S(2)}, u32[]{:S(2)}) %all-to-all-start.1) | async-done | bytes 1048608 | tf_op jit(solution)/shard_map/all_to_all | solution.py:33
  102.0 1.7 copy.49
  103.7 2.4 reshape.52
  106.1 1.4 convert_reduce_fusion
  108.1 3.2 bitcast_divide_fusion
  111.3 3.9 %copy.35 = f32[1,1024,8,64]{3,2,0,1:T(8,128)} copy(f32[1,1024,8,64]{1,3,2,0:T(8,128)} %bitcast_divide_fusion) | data formatting | bytes 4194304 | tf_op jit(solution)/shard_map/div | solution.py:24
  115.2 5.9 %reshape.56 = f32[8,1,65536]{2,1,0:T(1,128)S(1)} reshape(f32[1024,1,8,64]{3,2,1,0:T(8,128)} %bitcast.69) | data formatting | bytes 4194304
  121.2 52.2 %all_to_all.55 = f32[8,1,65536]{2,1,0:T(1,128)} all-to-all(f32[8,1,65536]{2,1,0:T(1,128)S(1)} %reshape.56), channel_id=1, replica_groups=mesh['batch'=4,'ctx'=8] {'ctx'}, dimensions={0} | all-to-all | bytes 4194304 | tf_op jit(solution)/shard_map/all_to_all | solution.py:41
  173.9 7.2 %reduce.2 = f32[8,65536]{1,0:T(8,128)S(1)} reduce(f32[8,1,65536]{2,1,0:T(1,128)} %all_to_all.55, f32[]{:T(128)} %broadcast.21), dimensions={1}, to_apply=%all_to_all.49.reduce_sub_computation | reduce | bytes 4194308 | tf_op jit(solution)/shard_map/all_to_all | solution.py:41
  181.1 3.7 %reshape.57 = f32[1024,1,8,64]{3,2,1,0:T(8,128)} reshape(f32[8,65536]{1,0:T(8,128)S(1)} %reduce.2) | data formatting | bytes 4194304
  184.8 2.8 copy.36
  188.4 120.6 %all-gather.2.cloned.1.call-done = bf16[4096,4096]{1,0:T(8,128)(2,1)} async-done(((bf16[1024,4096]{1,0:T(8,128)(2,1)}), bf16[4096,4096]{1,0:T(8,128)(2,1)}) %all-gather.2.cloned.1.call-update) | async-done | bytes 33554448 | tf_op jit(solution)/shard_map/all_gather | solution.py:47
  309.0 14.0 %fusion = bf16[1,128,4096]{2,1,0:T(8,128)(2,1)} fusion(bf16[128,4096]{0,1:T(8,128)(2,1)S(1)} %bitcast.73, bf16[4096,4096]{1,0:T(8,128)(2,1)} %all-gather.2.cloned.1.call-done), kind=kOutput, calls=%fused_computation.3 | convolution fusion | flops 4295491584 | bytes 35651584 | tf_op jit(solution)/shard_map/btw,wv->btv/dot_general | solution.py:44
  (14 shorter events, 2.3 us)
Async XLA Ops:
  6.5 1.2 copy-start
  6.5 302.5 %all-gather.2.cloned.1.call-start = ((), (), s32[]{:S(2)}) async-start(), calls=%async_computation.4 | async-start | bytes 41943040 | tf_op jit(solution)/shard_map/all_gather | solution.py:47
  10.0 6.5 %copy-start.1 = (bf16[1,128,64,64]{1,3,2,0:T(8,128)(2,1)S(1)}, bf16[1,128,64,64]{1,3,2,0:T(8,128)(2,1)}, u32[]{:S(2)}) copy-start(bf16[1,128,64,64]{1,3,2,0:T(8,128)(2,1)} %param.5) | copy-start | bytes 3145732
  10.0 33.0 %all-to-all-start.2 = ((bf16[1,128,64,64]{1,3,0,2:T(8,128)(2,1)}), bf16[1,128,64,64]{1,3,0,2:T(8,128)(2,1)S(1)}, u32[]{:S(2)}, u32[]{:S(2)}) async-start(bf16[1,128,64,64]{1,3,0,2:T(8,128)(2,1)} %fusion.10), calls=%async_computation.2 | async-start | bytes 2097152 | tf_op jit(solution)/shard_map/all_to_all | solution.py:31
  72.0 30.1 %all-to-all-start.1 = ((bf16[1,128,64,64]{1,3,0,2:T(8,128)(2,1)}), bf16[1,128,64,64]{1,3,0,2:T(8,128)(2,1)S(1)}, u32[]{:S(2)}, u32[]{:S(2)}) async-start(bf16[1,128,64,64]{1,3,0,2:T(8,128)(2,1)} %bitcast.81), calls=%async_computation.1 | async-start | bytes 2097152 | tf_op jit(solution)/shard_map/all_to_all | solution.py:33
  103.7 4.3 %copy-start.2 = (bf16[1024,8,64]{0,2,1:T(8,128)(2,1)S(1)}, bf16[1024,8,64]{0,2,1:T(8,128)(2,1)}, u32[]{:S(2)}) copy-start(bf16[1024,8,64]{0,2,1:T(8,128)(2,1)} %reshape.51) | copy-start | bytes 3145732
Sparse Core Ops, SparseCore 0:
  9.2 299.7 all-gather.1
where the time goes:
time: 331 us; the launch traced here: 330 us
  waiting for transfers between devices  166 us (50%)
  blocking collectives  81.2 us (25%)
  local copies, waits for them, and re-layouts  29.2 us (9%)
  matrix products  17.8 us (5%)
  between operations  13.5 us (4%)
  other arithmetic  12.3 us (4%)
  starting transfers between devices  10 us (3%)
    all_gather x1, waiting for transfers between devices, shards(): lax.all_gather(out_weight, 'batch', axis=0, tiled=True)  121 us
    all_to_all x1, blocking collectives, shards(): lax.all_to_all(head_read, 'ctx', split_axis=1, concat_axis=2, tiled=True)  52.2 us
    all_to_all x1, blocking collectives, shards(): lax.all_to_all(key_feature, 'ctx', split_axis=2, concat_axis=1, tiled=True)  29 us
    all_to_all x1, waiting for transfers between devices, shards(): lax.all_to_all(query_feature, 'ctx', split_axis=2, concat_axis=1, tiled=T...  25.3 us
    all_to_all x1, waiting for transfers between devices, shards(): lax.all_to_all(contents, 'ctx', split_axis=2, concat_axis=1, tiled=True)  19.3 us
    dot_general x1, matrix products, shards(): jnp.einsum('btw,wv->btv', mixed, lax.all_gather(out_weight, 'batch', axis...  14 us
    unnamed x9, local copies, waits for them, and re-layouts  10.4 us
    all_to_all x1, other arithmetic, shards(): lax.all_to_all(head_read, 'ctx', split_axis=1, concat_axis=2, tiled=True)  7.22 us
  transfers between devices with their start and end apart: 3, of which 3 were waited for; matrix products, arithmetic and copies ran while one was open for 14% of the time, Pallas kernels for 0%

commit v1 on v0

--- a/solution.py
+++ b/solution.py
@@ -2,6 +2,22 @@
 import jax.numpy as jnp
 from jax import lax
 from jax.sharding import PartitionSpec as P
+
+
+def summed_both_ways(x, axis, dim, term):
+    size, here, rows = (lax.axis_size(axis), lax.axis_index(axis), x.shape[dim])
+    right = [(i, (i + 1) % size) for i in range(size)]
+    left = [(i, (i - 1) % size) for i in range(size)]
+    middle = size // 2
+    from_left = from_right = x
+    subtotal = term(x, here * rows)
+    for step in range(1, middle + 1):
+        from_left = lax.ppermute(from_left, axis, right)
+        if step < size - middle:
+            from_right = lax.ppermute(from_right, axis, left)
+            subtotal = subtotal + term(from_right, (here + step) % size * rows)
+        subtotal = subtotal + term(from_left, (here - step) % size * rows)
+    return subtotal
 
 
 def to_features(values):
@@ -41,11 +57,16 @@
     read = lax.all_to_all(head_read, "ctx", split_axis=1, concat_axis=2, tiled=True)
     mixed = after_reading(read, count)
     mixed = mixed.reshape(mixed.shape[0], mixed.shape[1], -1)
-    return jnp.einsum(
-        "btw,wv->btv",
-        mixed,
-        lax.all_gather(out_weight, "batch", axis=0, tiled=True),
-        preferred_element_type=jnp.float32,
+    return summed_both_ways(
+        out_weight,
+        "batch",
+        0,
+        lambda part, at: jnp.einsum(
+            "btw,wv->btv",
+            lax.dynamic_slice_in_dim(mixed, at, part.shape[0], axis=2),
+            part,
+            preferred_element_type=jnp.float32,
+        ),
     ).astype(jnp.bfloat16)
 
 

time: 331 us -> 551 us (1.66)
  waiting for transfers between devices: 166 us -> 458 us
  blocking collectives: 81.2 us -> 0 us
  between operations: 13.5 us -> 0.11 us
  starting transfers between devices: 10 us -> 22.4 us
  matrix products: 17.8 us -> 23.5 us
    ppermute x0 -> x3, waiting for transfers between devices: none -> 360 us  [the longest x2 283 us: summed_both_ways(): from_left = lax.ppermute(from_left, axis, right)]
    all_gather x1 -> x0, waiting for transfers between devices: 121 us -> none  [shards(): lax.all_gather(out_weight, 'batch', axis=0, tiled=True)]
    all_to_all x2 -> x0, blocking collectives: 81.2 us -> none  [the longest x1 52.2 us: shards(): lax.all_to_all(head_read, 'ctx', split_axis=1, concat_axis=2, tiled=True)]
    all_to_all x0 -> x2, waiting for transfers between devices: none -> 74 us  [the longest x1 49 us: shards(): lax.all_to_all(head_read, 'ctx', split_axis=1, concat_axis=2, tiled=True)]
    all_to_all x1, waiting for transfers between devices: 19.3 us -> 0.01 us  [shards(): lax.all_to_all(contents, 'ctx', split_axis=2, concat_axis=1, tiled=True)]
    all_to_all x0 -> x2, starting transfers between devices: none -> 8.44 us  [the longest x1 4.88 us: shards(): lax.all_to_all(head_read, 'ctx', split_axis=1, concat_axis=2, tiled=True)]
    dot_general x1 -> x4, matrix products: 14 us -> 19.7 us  [shards(): jnp.einsum('btw,wv->btv', lax.dynamic_slice_in_dim(mixed, at, part.shape[...]
    ppermute x0 -> x3, starting transfers between devices: none -> 5.52 us  [the longest x2 4.03 us: summed_both_ways(): from_left = lax.ppermute(from_left, axis, right)]
  transfers between devices with their start and end apart: 3 -> 7, of which waited for: 3 -> 6; matrix products, arithmetic and copies ran while one was open for 14% -> 11% of each run, Pallas kernels for 0% -> 0%
where the time goes in v1:
time: 551 us; the launch traced here: 550 us
  waiting for transfers between devices  458 us (83%)
  local copies, waits for them, and re-layouts  31.4 us (6%)
  matrix products  23.5 us (4%)
  starting transfers between devices  22.4 us (4%)
  other arithmetic  14.5 us (3%)
    ppermute x2, waiting for transfers between devices, summed_both_ways(): from_left = lax.ppermute(from_left, axis, right)  283 us
    ppermute x1, waiting for transfers between devices, summed_both_ways(): from_right = lax.ppermute(from_right, axis, left)  76.5 us
    all_to_all x1, waiting for transfers between devices, shards(): lax.all_to_all(head_read, 'ctx', split_axis=1, concat_axis=2, tiled=True)  49 us
    all_to_all x1, waiting for transfers between devices, shards(): lax.all_to_all(key_feature, 'ctx', split_axis=2, concat_axis=1, tiled=True)  25 us
    all_to_all x1, waiting for transfers between devices, shards(): lax.all_to_all(query_feature, 'ctx', split_axis=2, concat_axis=1, tiled=T...  24.4 us
    dot_general x4, matrix products, shards(): jnp.einsum('btw,wv->btv', lax.dynamic_slice_in_dim(mixed, at, part.shape[...  19.7 us
    unnamed x9, local copies, waits for them, and re-layouts  12.5 us
  transfers between devices with their start and end apart: 7, of which 6 were waited for; matrix products, arithmetic and copies ran while one was open for 11% of the time, Pallas kernels for 0%

profile of v1, /device:TPU:0, one launch (start us, length us, event | category | flops | bytes accessed | tf_op | source)
XLA Modules:
  0.0 549.9 jit_solution(6972778825171388220)
XLA Ops:
  0.0 3.0 collective-permute-start.1
  3.0 3.4 fusion.11
  6.4 4.9 all-to-all-start.2
  13.5 24.4 %all-to-all-done.2 = bf16[1,128,64,64]{1,3,0,2:T(8,128)(2,1)S(1)} async-done(((bf16[1,128,64,64]{1,3,0,2:T(8,128)(2,1)}), bf16[1,128,64,64]{1,3,0,2:T(8,128)(2,1)S(1)}, u32[]{:S(2)}, u32[]{:S(2)}) %all-to-all-start.2) | async-done | bytes 1048608 | tf_op jit(solution)/shard_map/all_to_all | solution.py:47
  37.8 3.6 all-to-all-start
  42.9 25.0 %all-to-all-done = bf16[1,128,64,64]{1,3,0,2:T(8,128)(2,1)S(1)} async-done(((bf16[1,128,64,64]{1,3,0,2:T(8,128)(2,1)}), bf16[1,128,64,64]{1,3,0,2:T(8,128)(2,1)S(1)}, u32[]{:S(2)}, u32[]{:S(2)}) %all-to-all-start) | async-done | bytes 1048608 | tf_op jit(solution)/shard_map/all_to_all | solution.py:48
  67.9 3.6 all-to-all-start.1
  71.4 114.1 %collective-permute-done.1 = bf16[1024,4096]{1,0:T(8,128)(2,1)} collective-permute-done((bf16[1024,4096]{1,0:T(8,128)(2,1)}, bf16[1024,4096]{1,0:T(8,128)(2,1)}, u32[]{:S(2)}, u32[]{:S(2)}) %collective-permute-start.1) | collective-permute-done | bytes 8388640 | tf_op jit(solution)/shard_map/ppermute | solution.py:15
  191.5 2.3 reshape.79
  195.5 2.4 reshape.80
  199.9 3.2 bitcast_divide_fusion
  203.1 3.8 copy.35
  206.9 7.2 %reshape.88 = f32[8,1,65536]{2,1,0:T(1,128)} reshape(f32[1024,1,8,64]{3,2,1,0:T(8,128)} %bitcast.83) | data formatting | bytes 4194304
  214.2 4.9 all-to-all-start.3
  219.0 49.0 %all-to-all-done.3 = f32[8,1,65536]{2,1,0:T(1,128)S(1)} async-done(((f32[8,1,65536]{2,1,0:T(1,128)}), f32[8,1,65536]{2,1,0:T(1,128)S(1)}, u32[]{:S(2)}, u32[]{:S(2)}) %all-to-all-start.3) | async-done | bytes 2097184 | tf_op jit(solution)/shard_map/all_to_all | solution.py:57
  269.9 7.2 %reduce.2 = f32[8,65536]{1,0:T(8,128)S(1)} reduce(f32[8,1,65536]{2,1,0:T(1,128)} %copy-done, f32[]{:T(128)} %broadcast.29), dimensions={1}, to_apply=%all_to_all.49.reduce_sub_computation | reduce | bytes 4194308 | tf_op jit(solution)/shard_map/all_to_all | solution.py:57
  277.2 3.6 reshape.89
  280.8 3.0 copy.36
  284.6 4.7 fusion.16
  289.3 76.5 %collective-permute-done = bf16[1024,4096]{1,0:T(8,128)(2,1)} collective-permute-done((bf16[1024,4096]{1,0:T(8,128)(2,1)}, bf16[1024,4096]{1,0:T(8,128)(2,1)}, u32[]{:S(2)}, u32[]{:S(2)}) %collective-permute-start) | collective-permute-done | bytes 8388640 | tf_op jit(solution)/shard_map/ppermute | solution.py:17
  365.8 4.7 convolution_add_fusion.2
  370.6 4.7 convolution_add_fusion.1
  375.2 169.0 %collective-permute-done.2 = bf16[1024,4096]{1,0:T(8,128)(2,1)} collective-permute-done((bf16[1024,4096]{1,0:T(8,128)(2,1)}, bf16[1024,4096]{1,0:T(8,128)(2,1)}, u32[]{:S(2)}, u32[]{:S(2)}) %collective-permute-start.2) | collective-permute-done | bytes 8388640 | tf_op jit(solution)/shard_map/ppermute | solution.py:15
  544.2 5.6 %fusion.1 = bf16[1,128,4096]{2,1,0:T(8,128)(2,1)} fusion(f32[128,4096]{1,0:T(8,128)S(1)} %convolution_add_fusion.1, bf16[1024,4096]{1,0:T(8,128)(2,1)} %collective-permute-done.2, bf16[1,128,4096]{1,2,0:T(8,128)(2,1)S(1)} %bitcast.90, s32[]{:T(128)S(6)} %select_n.42), kind=kOutput, calls=%fused_computation.6 | convolution fusion | flops 1074790400 | bytes 11796484 | tf_op jit(solution)/shard_map/btw,wv->btv/dot_general | solution.py:64
  (22 shorter events, 15.9 us)
Async XLA Ops:
  0.0 11.3 %copy-start.1 = (bf16[1,128,64,64]{1,3,2,0:T(8,128)(2,1)S(1)}, bf16[1,128,64,64]{1,3,2,0:T(8,128)(2,1)}, u32[]{:S(2)}) copy-start(bf16[1,128,64,64]{1,3,2,0:T(8,128)(2,1)} %param.5) | copy-start | bytes 3145732
  0.0 185.5 %collective-permute-start.1 = (bf16[1024,4096]{1,0:T(8,128)(2,1)}, bf16[1024,4096]{1,0:T(8,128)(2,1)}, u32[]{:S(2)}, u32[]{:S(2)}) collective-permute-start(bf16[1024,4096]{1,0:T(8,128)(2,1)} %param.7), channel_id=1, source_target_pairs={{0,8},{8,16},{16,24},{24,0},{1,9},{9,17},{17,25},{25,1},{2,10},{10... | collective-permute-start | bytes 25165832 | tf_op jit(solution)/shard_map/ppermute | solution.py:15
  6.4 31.4 %all-to-all-start.2 = ((bf16[1,128,64,64]{1,3,0,2:T(8,128)(2,1)}), bf16[1,128,64,64]{1,3,0,2:T(8,128)(2,1)S(1)}, u32[]{:S(2)}, u32[]{:S(2)}) async-start(bf16[1,128,64,64]{1,3,0,2:T(8,128)(2,1)} %fusion.11), calls=%async_computation.2 | async-start | bytes 2097152 | tf_op jit(solution)/shard_map/all_to_all | solution.py:47
  37.8 30.1 %all-to-all-start = ((bf16[1,128,64,64]{1,3,0,2:T(8,128)(2,1)}), bf16[1,128,64,64]{1,3,0,2:T(8,128)(2,1)S(1)}, u32[]{:S(2)}, u32[]{:S(2)}) async-start(bf16[1,128,64,64]{1,3,0,2:T(8,128)(2,1)} %fusion.10), calls=%async_computation | async-start | bytes 2097152 | tf_op jit(solution)/shard_map/all_to_all | solution.py:48
  41.4 324.4 %collective-permute-start = (bf16[1024,4096]{1,0:T(8,128)(2,1)}, bf16[1024,4096]{1,0:T(8,128)(2,1)}, u32[]{:S(2)}, u32[]{:S(2)}) collective-permute-start(bf16[1024,4096]{1,0:T(8,128)(2,1)} %param.7), channel_id=1, source_target_pairs={{0,24},{8,0},{16,8},{24,16},{1,25},{9,1},{17,9},{25,17},{2,26},{10... | collective-permute-start | bytes 25165832 | tf_op jit(solution)/shard_map/ppermute | solution.py:17
  67.9 125.9 %all-to-all-start.1 = ((bf16[1,128,64,64]{1,3,0,2:T(8,128)(2,1)}), bf16[1,128,64,64]{1,3,0,2:T(8,128)(2,1)S(1)}, u32[]{:S(2)}, u32[]{:S(2)}) async-start(bf16[1,128,64,64]{1,3,0,2:T(8,128)(2,1)} %bitcast.98), calls=%async_computation.1 | async-start | bytes 2097152 | tf_op jit(solution)/shard_map/all_to_all | solution.py:49
  185.5 358.7 %collective-permute-start.2 = (bf16[1024,4096]{1,0:T(8,128)(2,1)}, bf16[1024,4096]{1,0:T(8,128)(2,1)}, u32[]{:S(2)}, u32[]{:S(2)}) collective-permute-start(bf16[1024,4096]{1,0:T(8,128)(2,1)} %collective-permute-done.1), channel_id=1, source_target_pairs={{0,8},{8,16},{16,24},{24,0},{1,9},{9,17},{17,25},{25,1},{2,10},{10... | collective-permute-start | bytes 25165832 | tf_op jit(solution)/shard_map/ppermute | solution.py:15
  195.5 4.4 copy-start.2
  214.2 53.9 %all-to-all-start.3 = ((f32[8,1,65536]{2,1,0:T(1,128)}), f32[8,1,65536]{2,1,0:T(1,128)S(1)}, u32[]{:S(2)}, u32[]{:S(2)}) async-start(f32[8,1,65536]{2,1,0:T(1,128)} %reshape.88), calls=%async_computation.3 | async-start | bytes 4194304 | tf_op jit(solution)/shard_map/all_to_all | solution.py:57
  268.1 1.4 copy-start
